TPU v7x, 32 devices: a whole 2x2x4 slice. The times are simulated.
32 devices in a mesh: leaf: 8 (over z, x), blk: 4 (over y, core).
Axes of the slice: x: 2, y: 2, z: 4, core: 2. Of those that a mesh axis runs over, the one named last changes fastest.
Arguments:
- desc_panel: bfloat16 [256, 384, 128], P(('leaf', 'blk')), may hold values from -18 to 18
- row_map: int32 [256, 3], P(('leaf', 'blk')), may hold values from 0 to 55, as said below
- anc_order: int32 [8], replicated, may hold values from 0 to 7, as said below
- anc_below: int32 [8, 12], replicated, may hold values from 32 to 55, as said below
- anc_panel: float32 [8, 4, 4, 128, 512], P('leaf', None, 'blk'), may hold values from -6 to 27, as said below
Outputs:
- chol_panel: float32 [8, 4, 4, 128, 512], P('leaf', None, 'blk')
Inputs may be any that keep to these rules, and one draw needn't show every extreme that they name: `row_map`: entry 0 of each row is a column block of one ancestor; the other entries are distinct entries of that ancestor's row of anc_below. Over the descendants of one device, entry 0 names the column blocks of any one ancestor at most 2 times, and of some ancestor exactly 2 times. `anc_order`: each leaf index holds a different column range. `anc_below`: each row holds 12 distinct indices. `anc_panel`: the leading 512 rows of each ancestor's panel are symmetric, and the leading block of S stays positive definite.
All inputs are finite; a program needn't handle non-finite values.
Results may differ from a plain program's by a relative error of at most 0.0003.
Values may be sent and summed in bfloat16 or wider, within the bound.
A program may use at most 192 MiB of HBM per device.

v0:
```python
import jax
import jax.numpy as jnp
from jax import lax
from jax.sharding import PartitionSpec as P

SLOTS = 2
slot_group = 16


def leaf_owner(ranges, anc_order):
    leaves = jnp.arange(anc_order.shape[0], dtype=jnp.int32)
    return jnp.sum(jnp.where(anc_order[None, :] == ranges[:, None], leaves[None, :], 0), axis=1)


def block_positions(block_ids, owner_leaf, anc_order, anc_below, column_blocks, position_count):
    column_base = anc_order[owner_leaf] * column_blocks
    relative = block_ids - column_base[:, None]
    in_columns = (relative >= 0) & (relative < column_blocks)
    below_ids = anc_below[owner_leaf]
    matching = block_ids[:, :, None] == below_ids[:, None, :]
    offsets = column_blocks + jnp.arange(below_ids.shape[1], dtype=jnp.int32)
    below_place = jnp.sum(jnp.where(matching, offsets[None, None, :], 0), axis=2)
    located = jnp.any(matching, axis=2)
    return jnp.where(in_columns, relative, jnp.where(located, below_place, position_count))


def place_blocks(running, group_place, group_products):
    return running + jnp.einsum(
        "kq,kxy->qxy", group_place, group_products, precision=lax.Precision.HIGHEST
    )


def shards(desc_panel, row_map, anc_order, anc_below, anc_panel):
    leaf_count = lax.axis_size("leaf")
    blk_count = lax.axis_size("blk")
    desc_count, block_count = row_map.shape
    block_rows = anc_panel.shape[3]
    panel_width = anc_panel.shape[4]
    wide_desc = desc_panel.shape[2]
    column_blocks = panel_width // block_rows
    position_count = column_blocks + anc_below.shape[1]
    slot_count = leaf_count * SLOTS
    group_count = slot_count // slot_group
    owner_leaf = leaf_owner(row_map[:, 0] // column_blocks, anc_order)
    positions = block_positions(
        row_map, owner_leaf, anc_order, anc_below, column_blocks, position_count
    )
    desc_index = jnp.arange(desc_count, dtype=jnp.int32)
    same_owner = owner_leaf[:, None] == owner_leaf[None, :]
    earlier = desc_index[None, :] < desc_index[:, None]
    ranking = jnp.sum(same_owner & earlier, axis=1)
    slot_of = owner_leaf * SLOTS + ranking
    matches = slot_of[None, :] == jnp.arange(slot_count, dtype=jnp.int32)[:, None]
    filled = jnp.any(matches, axis=1)
    chosen = jnp.sum(jnp.where(matches, desc_index[None, :], 0), axis=1)
    picked = jnp.where(filled, chosen, desc_count)
    slot_codes = jnp.where(filled[:, None], positions[chosen], position_count).reshape(
        leaf_count, SLOTS, block_count
    )
    send_rows = jnp.take(desc_panel, picked, axis=0, mode="fill", fill_value=0)
    send_rows = send_rows.reshape(leaf_count, SLOTS, block_count * block_rows, wide_desc)
    received, received_codes = (
        lax.all_to_all(send_rows, "leaf", split_axis=0, concat_axis=0, tiled=True),
        lax.all_to_all(
            slot_codes.astype(jnp.bfloat16), "leaf", split_axis=0, concat_axis=0, tiled=True
        ),
    )
    slot_data = received.reshape(group_count, slot_group, block_count * block_rows, wide_desc)

    def accumulate(running, element):
        group_data, group_place = element
        products = jnp.einsum(
            "kaw,kyw->kay",
            group_data,
            group_data[:, :block_rows],
            preferred_element_type=jnp.float32,
        )
        products = products.reshape(slot_group * block_count, block_rows, block_rows)
        return (place_blocks(running, group_place, products), None)

    codes_int = received_codes.astype(jnp.int32).reshape(slot_count, block_count)
    target = codes_int * column_blocks + codes_int[:, :1]
    placing = (
        target[:, :, None]
        == jnp.arange(position_count * column_blocks, dtype=jnp.int32)[None, None, :]
    ).astype(jnp.float32)
    placing = placing.reshape(group_count, slot_group * block_count, position_count * column_blocks)
    initial = jnp.zeros((position_count * column_blocks, block_rows, block_rows), jnp.float32)
    running, _ = lax.scan(accumulate, initial, (slot_data, placing))
    update = running.reshape(position_count, column_blocks, block_rows, block_rows).transpose(
        0, 2, 1, 3
    )
    update = update.reshape(position_count // blk_count, blk_count, block_rows, panel_width)
    local_rows = anc_panel[0]
    mine = lax.axis_index("blk")
    marker = (jnp.arange(blk_count, dtype=jnp.int32) == mine).astype(jnp.float32)
    combined = update - local_rows * marker[None, :, None, None]
    summed = lax.psum(combined, "blk")
    diagonal = -summed.reshape(position_count * block_rows, panel_width)[:panel_width]
    own_rows = -lax.dynamic_slice_in_dim(summed, mine, 1, 1)
    lower_factor = jnp.linalg.cholesky(diagonal)
    panel_rows = own_rows.reshape(-1, panel_width)
    solved = jax.scipy.linalg.solve_triangular(lower_factor, panel_rows.T, lower=True).T
    return solved.reshape(anc_panel.shape)


def solution(mesh):
    in_specs = (
        P(("leaf", "blk"), None, None),
        P(("leaf", "blk"), None),
        P(),
        P(),
        P("leaf", None, "blk", None, None),
    )
    out_specs = P("leaf", None, "blk", None, None)
    return jax.shard_map(shards, mesh=mesh, in_specs=in_specs, out_specs=out_specs, check_vma=False)
```

profile of v0, /device:TPU:0, one launch (start us, length us, event | category | flops | bytes accessed | tf_op | source)
XLA Modules:
  0.0 327.3 jit_solution(11401863305329569041)
XLA Ops:
  6.5 0.8 fusion.45
  7.3 0.8 select_reduce_fusion.5
  8.5 0.8 copy.53
  9.4 1.3 gather_fusion
  10.7 1.2 gather_fusion.1
  11.9 0.9 compare_reduce_fusion
  12.8 0.9 fusion.40
  14.8 0.7 copy.58
  15.5 7.3 %all-to-all-start = ((bf16[8,2,3]{2,1,0:T(2,128)(2,1)}), bf16[8,2,3]{2,1,0:T(2,128)(2,1)S(1)}, u32[]{:S(2)}, u32[]{:S(2)}) async-start(bf16[8,2,3]{2,1,0:T(2,128)(2,1)} %copy.58), calls=%async_computation | async-start | bytes 8192 | tf_op jit(solution)/shard_map/all_to_all | solution.py:64
  22.8 0.9 gather_fusion.3
  23.7 1.3 broadcast_select_fusion
  25.0 4.1 %all-to-all-done = bf16[8,2,3]{2,1,0:T(2,128)(2,1)S(1)} async-done(((bf16[8,2,3]{2,1,0:T(2,128)(2,1)}), bf16[8,2,3]{2,1,0:T(2,128)(2,1)S(1)}, u32[]{:S(2)}, u32[]{:S(2)}) %all-to-all-start) | async-done | bytes 128 | tf_op jit(solution)/shard_map/all_to_all | solution.py:64
  29.2 3.6 %all-to-all-start.1 = ((bf16[8,2,384,128]{3,2,1,0:T(8,128)(2,1)}), bf16[8,2,384,128]{3,2,1,0:T(8,128)(2,1)S(1)}, u32[]{:S(2)}, u32[]{:S(2)}) async-start(bf16[8,2,384,128]{3,2,1,0:T(8,128)(2,1)} %broadcast_select_fusion), calls=%async_computation.1 | async-start | bytes 3145728 | tf_op jit(solution)/shard_map/all_to_all | solution.py:63
  32.8 1.6 copy.62
  34.8 33.9 %all-to-all-done.1 = bf16[8,2,384,128]{3,2,1,0:T(8,128)(2,1)S(1)} async-done(((bf16[8,2,384,128]{3,2,1,0:T(8,128)(2,1)}), bf16[8,2,384,128]{3,2,1,0:T(8,128)(2,1)S(1)}, u32[]{:S(2)}, u32[]{:S(2)}) %all-to-all-start.1) | async-done | bytes 1572896 | tf_op jit(solution)/shard_map/all_to_all | solution.py:63
  69.3 6.0 %fusion.3 = f32[16,128,4,128]{3,0,1,2:T(8,128)} fusion(f32[48,128,128]{2,1,0:T(8,128)S(1)} %bitcast.107, s32[16,4]{0,1:T(4,128)S(1)} %multiply_add_fusion, s32[48]{0:T(128)S(1)} %add.130), kind=kOutput, calls=%fused_computation.10 | convolution fusion | flops 603982848 | bytes 7340480 | tf_op jit(solution)/shard_map/while/body/eval_jaxpr/kq,kxy->qxy/dot_general | solution.py:28
  75.3 5.7 %copy.61 = f32[16,128,4,128]{1,3,2,0:T(8,128)} copy(f32[16,128,4,128]{3,0,1,2:T(8,128)} %fusion.3) | data formatting | bytes 8388608 | tf_op jit(solution)/shard_map/transpose | solution.py:90
  80.9 4.7 %multiply_subtract_fusion = f32[4,4,128,512]{2,3,1,0:T(8,128)} fusion(f32[4,4,128,512]{2,3,1,0:T(8,128)} %bitcast.106, f32[4]{0:T(128)S(1)} %compare_convert_fusion, f32[4,128,512]{1,2,0:T(8,128)S(1)} %copy.62), kind=kLoop, calls=%fused_computation.6 | loop fusion | flops 2097152 | bytes 9437200 | tf_op jit(solution)/shard_map/sub | solution.py:97
  85.7 84.5 %all-reduce.3.cloned.1.call-done = f32[4,4,128,512]{2,3,1,0:T(8,128)} async-done(((f32[4,4,128,512]{2,3,1,0:T(8,128)}), f32[4,4,128,512]{2,3,1,0:T(8,128)}) %all-reduce.3.cloned.1.call-update) | async-done | bytes 4194320 | tf_op jit(solution)/shard_map/psum | solution.py:98
  170.1 1.3 slice_negate_fusion
  171.4 0.7 copy.63
  172.1 1.0 copy.84
  173.2 1.6 copy.64
  175.0 1.0 copy-done.2
  175.9 11.7 %cholesky.104 = f32[128,128]{1,0:T(8,128)S(1)} custom-call(f32[128,128]{1,0:T(8,128)S(1)} %cholesky.266), custom_call_target="Cholesky" | custom-call | tf_op jit(solution)/shard_map/jit(cholesky)/cholesky | solution.py:101
  187.8 9.8 %custom-call.31 = f32[1,128,128]{1,2,0:T(8,128)S(1)} custom-call(f32[1,128,128]{2,1,0:T(8,128)S(1)} %get-tuple-element.44), custom_call_target="InvertDiagBlocksLowerTriangular" | custom-call | tf_op jit(solution)/shard_map/jit(cholesky)/cholesky | solution.py:101
  197.6 1.2 constant_dynamic-update-slice_fusion.3
  198.9 1.3 convolution_subtract_fusion.3
  200.1 11.9 %cholesky.217 = f32[128,128]{1,0:T(8,128)S(1)} custom-call(f32[128,128]{1,0:T(8,128)S(1)} %cholesky.270), custom_call_target="Cholesky" | custom-call | tf_op jit(solution)/shard_map/jit(cholesky)/cholesky | solution.py:101
  212.0 0.7 compare_reduce_fusion.3
  213.4 9.8 %custom-call.32 = f32[1,128,128]{1,2,0:T(8,128)S(1)} custom-call(f32[1,128,128]{2,1,0:T(8,128)S(1)} %get-tuple-element.41), custom_call_target="InvertDiagBlocksLowerTriangular" | custom-call | tf_op jit(solution)/shard_map/jit(cholesky)/cholesky | solution.py:101
  223.4 1.3 convolution_subtract_fusion.4
  224.7 11.7 %cholesky.238 = f32[128,128]{1,0:T(8,128)S(1)} custom-call(f32[128,128]{1,0:T(8,128)S(1)} %cholesky.275), custom_call_target="Cholesky" | custom-call | tf_op jit(solution)/shard_map/jit(cholesky)/cholesky | solution.py:101
  236.5 0.7 compare_reduce_fusion.2
  237.2 9.8 %custom-call.33 = f32[1,128,128]{1,2,0:T(8,128)S(1)} custom-call(f32[1,128,128]{2,1,0:T(8,128)S(1)} %get-tuple-element.38), custom_call_target="InvertDiagBlocksLowerTriangular" | custom-call | tf_op jit(solution)/shard_map/jit(cholesky)/cholesky | solution.py:101
  247.2 1.2 convolution_subtract_fusion.5
  248.5 11.9 %cholesky.255 = f32[128,128]{1,0:T(8,128)S(1)} custom-call(f32[128,128]{1,0:T(8,128)S(1)} %convolution_subtract_fusion.5), custom_call_target="Cholesky" | custom-call | tf_op jit(solution)/shard_map/jit(cholesky)/cholesky | solution.py:101
  263.8 7.9 %while.1 = (s32[]{:T(128)}, f32[512,512]{1,0:T(8,128)S(1)}, s32[4,2]{0,1:T(2,128)S(1)}, f32[4,128,128]{2,1,0:T(8,128)S(1)}, s32[]{:T(128)}) while((s32[]{:T(128)}, f32[512,512]{1,0:T(8,128)S(1)}, s32[4,2]{0,1:T(2,128)S(1)}, f32[4,128,128]{2,1,0:T(8,128)S(1)}, s32[]{:T(128)}) %tuple.30), condition=%wide.while_cond, body=%wide.while_body.sunk | while | flops 2 | bytes 131181 | solution.py:103
  264.4 1.4 bitcast_dynamic-update-slice_fusion.2
  266.4 1.4 bitcast_dynamic-update-slice_fusion.2
  268.3 1.4 bitcast_dynamic-update-slice_fusion.2
  270.3 1.4 bitcast_dynamic-update-slice_fusion.2
  271.7 39.3 %custom-call.34 = f32[4,128,128]{1,2,0:T(8,128)S(1)} custom-call(f32[4,128,128]{2,1,0:T(8,128)S(1)} %get-tuple-element.24), custom_call_target="InvertDiagBlocksLowerTriangular" | custom-call | tf_op jit(solution)/shard_map/jit(_solve_triangular)/triangular_solve | solution.py:103
  311.0 1.3 dynamic-slice_negate_fusion
  313.4 1.2 convolution_subtract_fusion.1
  315.1 1.3 convolution_subtract_fusion
  316.8 1.6 convolution_subtract_fusion.2
  318.9 1.3 copy.72
  (69 shorter events, 9.8 us)
Async XLA Ops:
  6.5 16.3 %copy-start = (bf16[8,384,128]{2,1,0:T(8,128)(2,1)S(1)}, bf16[8,384,128]{2,1,0:T(8,128)(2,1)}, u32[]{:S(2)}) copy-start(bf16[8,384,128]{2,1,0:T(8,128)(2,1)} %param.5) | copy-start | bytes 2359300
  15.5 13.7 %all-to-all-start = ((bf16[8,2,3]{2,1,0:T(2,128)(2,1)}), bf16[8,2,3]{2,1,0:T(2,128)(2,1)S(1)}, u32[]{:S(2)}, u32[]{:S(2)}) async-start(bf16[8,2,3]{2,1,0:T(2,128)(2,1)} %copy.58), calls=%async_computation | async-start | bytes 8192 | tf_op jit(solution)/shard_map/all_to_all | solution.py:64
  29.2 39.5 %all-to-all-start.1 = ((bf16[8,2,384,128]{3,2,1,0:T(8,128)(2,1)}), bf16[8,2,384,128]{3,2,1,0:T(8,128)(2,1)S(1)}, u32[]{:S(2)}, u32[]{:S(2)}) async-start(bf16[8,2,384,128]{3,2,1,0:T(8,128)(2,1)} %broadcast_select_fusion), calls=%async_computation.1 | async-start | bytes 3145728 | tf_op jit(solution)/shard_map/all_to_all | solution.py:63
  32.7 137.4 %all-reduce.3.cloned.1.call-start = ((), (), s32[]{:S(2)}) async-start(), calls=%async_computation.2 | async-start | bytes 8388608 | tf_op jit(solution)/shard_map/psum | solution.py:98
  174.9 1.0 copy-start.2
  271.7 39.3 %copy-start.1 = (f32[512,512]{1,0:T(8,128)}, f32[512,512]{1,0:T(8,128)S(1)}, u32[]{:S(2)}) copy-start(f32[512,512]{1,0:T(8,128)S(1)} %get-tuple-element.101) | copy-start | bytes 3145732
Sparse Core Ops, SparseCore 0:
  85.8 84.3 all-reduce.2
where the time goes:
time: 333 us; the launch traced here: 327 us
  other arithmetic  132 us (40%)
  waiting for transfers between devices  123 us (37%)
  local copies, waits for them, and re-layouts  27.7 us (8%)
  matrix products  17.8 us (5%)
  between operations  16.6 us (5%)
  starting transfers between devices  10.9 us (3%)
    psum x1, waiting for transfers between devices, shards(): summed = lax.psum(combined, 'blk')  84.5 us
    another operation x15, other arithmetic, shards(): lower_factor = jnp.linalg.cholesky(diagonal)  79.4 us
    another operation x3, other arithmetic, shards(): jax.scipy.linalg.solve_triangular(lower_factor, panel_rows.T, lower=True)  39.4 us
    all_to_all x1, waiting for transfers between devices, shards(): lax.all_to_all(send_rows, 'leaf', split_axis=0, concat_axis=0, tiled=True)  33.9 us
    another operation x12, local copies, waits for them, and re-layouts  7.81 us
    all_to_all x1, starting transfers between devices, shards(): lax.all_to_all(slot_codes.astype(jnp.bfloat16), 'leaf', split_axis=0, con...  7.28 us
  transfers between devices with their start and end apart: 3, of which 3 were waited for; matrix products, arithmetic and copies ran while one was open for 1% of the time, Pallas kernels for 0%

commit v1 on v0

--- a/solution.py
+++ b/solution.py
@@ -5,6 +5,29 @@
 
 SLOTS = 2
 slot_group = 16
+
+
+def split_up(x, dim, count):
+    before, after = (x.shape[:dim], x.shape[dim + 1 :])
+    return jnp.moveaxis(x.reshape(*before, count, -1, *after), dim, 0)
+
+
+def laid_out(blocks, dim):
+    blocks = jnp.moveaxis(blocks, 0, dim)
+    dims = blocks.shape
+    return blocks.reshape(*dims[:dim], dims[dim] * dims[dim + 1], *dims[dim + 2 :])
+
+
+def exchange_directly(array, axis, split_dim, concat_dim):
+    size, mine = (lax.axis_size(axis), lax.axis_index(axis))
+    blocks = split_up(array, split_dim, size)
+    out = blocks
+    for turn in range(1, size):
+        target, source = ((mine + turn) % size, (mine - turn) % size)
+        sent = lax.dynamic_index_in_dim(blocks, target, 0)
+        other = lax.ppermute(sent, axis, [(i, (i + turn) % size) for i in range(size)])
+        out = lax.dynamic_update_slice_in_dim(out, other, source, axis=0)
+    return laid_out(out, concat_dim)
 
 
 def leaf_owner(ranges, anc_order):
@@ -60,7 +83,7 @@
     send_rows = jnp.take(desc_panel, picked, axis=0, mode="fill", fill_value=0)
     send_rows = send_rows.reshape(leaf_count, SLOTS, block_count * block_rows, wide_desc)
     received, received_codes = (
-        lax.all_to_all(send_rows, "leaf", split_axis=0, concat_axis=0, tiled=True),
+        exchange_directly(send_rows, "leaf", 0, 0),
         lax.all_to_all(
             slot_codes.astype(jnp.bfloat16), "leaf", split_axis=0, concat_axis=0, tiled=True
         ),

time: 333 us -> 336 us (level)
  waiting for transfers between devices: 123 us -> 109 us
  starting transfers between devices: 10.9 us -> 18.6 us
  local copies, waits for them, and re-layouts: 27.7 us -> 34 us
    all_to_all x1 -> x0, waiting for transfers between devices: 33.9 us -> none  [shards(): lax.all_to_all(send_rows, 'leaf', split_axis=0, concat_axis=0, tiled=True)]
    ppermute x0 -> x7, starting transfers between devices: none -> 13.7 us  [exchange_directly(): lax.ppermute(sent, axis, [(i, (i + turn) % size) for i in range(size)])]
    ppermute x0 -> x7, waiting for transfers between devices: none -> 13.3 us  [exchange_directly(): lax.ppermute(sent, axis, [(i, (i + turn) % size) for i in range(size)])]
    psum x1, waiting for transfers between devices: 84.5 us -> 95.9 us  [shards(): summed = lax.psum(combined, 'blk')]
    all_to_all x1, waiting for transfers between devices: 4.13 us -> 0.01 us  [shards(): lax.all_to_all(slot_codes.astype(jnp.bfloat16), 'leaf', split_axis=0, con...]
    all_to_all x1 -> x0, starting transfers between devices: 3.58 us -> none  [shards(): lax.all_to_all(send_rows, 'leaf', split_axis=0, concat_axis=0, tiled=True)]
  transfers between devices with their start and end apart: 3 -> 9, of which waited for: 3 -> 5; matrix products, arithmetic and copies ran while one was open for 1% -> 3% of each run, Pallas kernels for 0% -> 0%
where the time goes in v1:
time: 336 us; the launch traced here: 329 us
  other arithmetic  132 us (39%)
  waiting for transfers between devices  109 us (32%)
  local copies, waits for them, and re-layouts  34 us (10%)
  matrix products  18.7 us (6%)
  starting transfers between devices  18.6 us (6%)
  between operations  17 us (5%)
    psum x1, waiting for transfers between devices, shards(): summed = lax.psum(combined, 'blk')  95.9 us
    another operation x15, other arithmetic, shards(): lower_factor = jnp.linalg.cholesky(diagonal)  79.4 us
    another operation x3, other arithmetic, shards(): jax.scipy.linalg.solve_triangular(lower_factor, panel_rows.T, lower=True)  40.3 us
    ppermute x7, starting transfers between devices, exchange_directly(): lax.ppermute(sent, axis, [(i, (i + turn) % size) for i in range(size)])  13.7 us
    ppermute x7, waiting for transfers between devices, exchange_directly(): lax.ppermute(sent, axis, [(i, (i + turn) % size) for i in range(size)])  13.3 us
    another operation x12, local copies, waits for them, and re-layouts  10.3 us
  transfers between devices with their start and end apart: 9, of which 5 were waited for; matrix products, arithmetic and copies ran while one was open for 3% of the time, Pallas kernels for 0%

profile of v1, /device:TPU:0, one launch (start us, length us, event | category | flops | bytes accessed | tf_op | source)
XLA Modules:
  0.0 329.1 jit_solution(17218874917717642073)
XLA Ops:
  8.7 1.9 gather_fusion.3
  10.7 1.6 broadcast_select_fusion
  12.9 3.0 collective-permute-start
  19.4 4.9 %all-to-all-start = ((bf16[8,2,3]{2,1,0:T(2,128)(2,1)}), bf16[8,2,3]{2,1,0:T(2,128)(2,1)S(1)}, u32[]{:S(2)}, u32[]{:S(2)}) async-start(bf16[8,2,3]{2,1,0:T(2,128)(2,1)} %copy.58), calls=%async_computation | async-start | bytes 8192 | tf_op jit(solution)/shard_map/all_to_all | solution.py:87
  24.5 1.6 copy.62
  26.2 2.0 constant_dynamic-slice_fusion.1
  28.2 1.8 collective-permute-start.1
  30.0 2.4 collective-permute-start.2
  32.7 1.5 collective-permute-start.3
  34.3 2.4 collective-permute-start.4
  36.6 1.5 collective-permute-start.5
  38.3 1.3 collective-permute-start.6
  39.6 1.0 constant_dynamic-update-slice_fusion.6
  40.5 9.7 %collective-permute-done.2 = bf16[1,1,2,384,128]{4,3,2,0,1:T(8,128)(2,1)} collective-permute-done((bf16[1,1,2,384,128]{4,3,2,0,1:T(8,128)(2,1)}, bf16[1,1,2,384,128]{4,3,2,0,1:T(8,128)(2,1)}, u32[]{:S(2)}, u32[]{:S(2)}) %collective-permute-start.2) | collective-permute-done | bytes 196640 | tf_op jit(solution)/shard_map/ppermute | solution.py:28
  50.2 1.0 constant_dynamic-update-slice_fusion.5
  51.1 2.1 collective-permute-done.3
  53.4 1.3 collective-permute-done.6
  55.3 6.0 %fusion.3 = f32[16,128,4,128]{3,0,1,2:T(8,128)} fusion(f32[48,128,128]{2,1,0:T(8,128)S(1)} %bitcast.108, s32[16,4]{0,1:T(4,128)S(1)} %multiply_add_fusion, s32[48]{0:T(128)S(1)} %add.244), kind=kOutput, calls=%fused_computation.10 | convolution fusion | flops 603982848 | bytes 7340480 | tf_op jit(solution)/shard_map/while/body/eval_jaxpr/kq,kxy->qxy/dot_general | solution.py:51
  61.4 5.7 %copy.61 = f32[16,128,4,128]{1,3,2,0:T(8,128)} copy(f32[16,128,4,128]{3,0,1,2:T(8,128)} %fusion.3) | data formatting | bytes 8388608 | tf_op jit(solution)/shard_map/transpose | solution.py:113
  67.0 4.7 %multiply_subtract_fusion = f32[4,4,128,512]{2,3,1,0:T(8,128)} fusion(f32[4,4,128,512]{2,3,1,0:T(8,128)} %bitcast.106, f32[4]{0:T(128)S(1)} %compare_convert_fusion, f32[4,128,512]{1,2,0:T(8,128)S(1)} %copy.62), kind=kLoop, calls=%fused_computation.6 | loop fusion | flops 2097152 | bytes 9437200 | tf_op jit(solution)/shard_map/sub | solution.py:120
  71.7 95.9 %all-reduce.3.cloned.1.call-done = f32[4,4,128,512]{2,3,1,0:T(8,128)} async-done(((f32[4,4,128,512]{2,3,1,0:T(8,128)}), f32[4,4,128,512]{2,3,1,0:T(8,128)}) %all-reduce.3.cloned.1.call-update) | async-done | bytes 4194320 | tf_op jit(solution)/shard_map/psum | solution.py:121
  167.6 1.3 slice_negate_fusion
  169.6 1.0 copy.84
  170.7 1.6 copy.64
  172.5 1.0 copy-done.3
  173.4 11.7 %cholesky.104 = f32[128,128]{1,0:T(8,128)S(1)} custom-call(f32[128,128]{1,0:T(8,128)S(1)} %cholesky.266), custom_call_target="Cholesky" | custom-call | tf_op jit(solution)/shard_map/jit(cholesky)/cholesky | solution.py:124
  185.3 9.8 %custom-call.31 = f32[1,128,128]{1,2,0:T(8,128)S(1)} custom-call(f32[1,128,128]{2,1,0:T(8,128)S(1)} %get-tuple-element.51), custom_call_target="InvertDiagBlocksLowerTriangular" | custom-call | tf_op jit(solution)/shard_map/jit(cholesky)/cholesky | solution.py:124
  195.1 1.2 constant_dynamic-update-slice_fusion
  196.4 1.3 convolution_subtract_fusion.3
  197.7 11.9 %cholesky.217 = f32[128,128]{1,0:T(8,128)S(1)} custom-call(f32[128,128]{1,0:T(8,128)S(1)} %cholesky.270), custom_call_target="Cholesky" | custom-call | tf_op jit(solution)/shard_map/jit(cholesky)/cholesky | solution.py:124
  210.9 9.8 %custom-call.32 = f32[1,128,128]{1,2,0:T(8,128)S(1)} custom-call(f32[1,128,128]{2,1,0:T(8,128)S(1)} %get-tuple-element.48), custom_call_target="InvertDiagBlocksLowerTriangular" | custom-call | tf_op jit(solution)/shard_map/jit(cholesky)/cholesky | solution.py:124
  220.9 1.3 convolution_subtract_fusion.4
  222.3 11.7 %cholesky.238 = f32[128,128]{1,0:T(8,128)S(1)} custom-call(f32[128,128]{1,0:T(8,128)S(1)} %cholesky.275), custom_call_target="Cholesky" | custom-call | tf_op jit(solution)/shard_map/jit(cholesky)/cholesky | solution.py:124
  234.7 9.8 %custom-call.33 = f32[1,128,128]{1,2,0:T(8,128)S(1)} custom-call(f32[1,128,128]{2,1,0:T(8,128)S(1)} %get-tuple-element.45), custom_call_target="InvertDiagBlocksLowerTriangular" | custom-call | tf_op jit(solution)/shard_map/jit(cholesky)/cholesky | solution.py:124
  244.7 1.2 convolution_subtract_fusion.5
  246.0 11.9 %cholesky.255 = f32[128,128]{1,0:T(8,128)S(1)} custom-call(f32[128,128]{1,0:T(8,128)S(1)} %convolution_subtract_fusion.5), custom_call_target="Cholesky" | custom-call | tf_op jit(solution)/shard_map/jit(cholesky)/cholesky | solution.py:124
  261.3 10.3 %while.1 = (s32[]{:T(128)}, f32[512,512]{1,0:T(8,128)S(1)}, s32[4,2]{0,1:T(2,128)S(1)}, f32[4,128,128]{2,1,0:T(8,128)}, s32[]{:T(128)}) while((s32[]{:T(128)}, f32[512,512]{1,0:T(8,128)S(1)}, s32[4,2]{0,1:T(2,128)S(1)}, f32[4,128,128]{2,1,0:T(8,128)}, s32[]{:T(128)}) %tuple.36), condition=%wide.while_cond, body=%wide.while_body.sunk | while | flops 2 | bytes 132705 | solution.py:126
  261.9 2.0 bitcast_dynamic-update-slice_fusion.2
  264.5 2.0 bitcast_dynamic-update-slice_fusion.2
  267.0 2.0 bitcast_dynamic-update-slice_fusion.2
  269.6 2.0 bitcast_dynamic-update-slice_fusion.2
  271.6 40.2 %custom-call.34 = f32[4,128,128]{1,2,0:T(8,128)S(1)} custom-call(f32[4,128,128]{2,1,0:T(8,128)} %get-tuple-element.24), custom_call_target="InvertDiagBlocksLowerTriangular" | custom-call | tf_op jit(solution)/shard_map/jit(_solve_triangular)/triangular_solve | solution.py:126
  311.8 1.4 dynamic-slice_negate_fusion
  314.3 1.2 convolution_subtract_fusion.1
  315.6 1.3 fusion.30
  316.8 1.3 convolution_subtract_fusion
  318.6 1.6 convolution_subtract_fusion.2
  320.7 1.3 copy.72
  (99 shorter events, 16.5 us)
Async XLA Ops:
  6.5 2.2 copy-start
  10.6 5.3 %copy-start.7 = (s32[8,3]{0,1:T(4,128)S(1)}, s32[8,3]{0,1:T(4,128)}, u32[]{:S(2)}) copy-start(s32[8,3]{0,1:T(4,128)} %param.6) | copy-start | bytes 292
  10.6 5.5 %copy-start.1 = (s32[8]{0:T(128)S(1)}, s32[8]{0:T(128)}, u32[]{:S(2)}) copy-start(s32[8]{0:T(128)} %param.7) | copy-start | bytes 100
  10.6 6.1 %copy-start.6 = (s32[8,12]{1,0:T(8,128)S(1)}, s32[8,12]{1,0:T(8,128)}, u32[]{:S(2)}) copy-start(s32[8,12]{1,0:T(8,128)} %param.8) | copy-start | bytes 1156
  12.9 13.2 %collective-permute-start = (bf16[1,1,2,384,128]{4,3,2,0,1:T(8,128)(2,1)}, bf16[1,1,2,384,128]{4,3,2,0,1:T(8,128)(2,1)}, u32[]{:S(2)}, u32[]{:S(2)}) collective-permute-start(bf16[1,1,2,384,128]{4,3,2,0,1:T(8,128)(2,1)} %constant_dynamic-slice_fusion.7), channel_id=1, source_target_pairs={{0,4},{4,8},{8,12},{12,16},{16,20},{20,24},{24,28},{28,0},{1,5},{5... | collective-permute-start | bytes 589832 | tf_op jit(solution)/shard_map/ppermute | solution.py:28
  19.4 13.0 %all-to-all-start = ((bf16[8,2,3]{2,1,0:T(2,128)(2,1)}), bf16[8,2,3]{2,1,0:T(2,128)(2,1)S(1)}, u32[]{:S(2)}, u32[]{:S(2)}) async-start(bf16[8,2,3]{2,1,0:T(2,128)(2,1)} %copy.58), calls=%async_computation | async-start | bytes 8192 | tf_op jit(solution)/shard_map/all_to_all | solution.py:87
  24.3 143.4 %all-reduce.3.cloned.1.call-start = ((), (), s32[]{:S(2)}) async-start(), calls=%async_computation.1 | async-start | bytes 8388608 | tf_op jit(solution)/shard_map/psum | solution.py:121
  28.2 10.1 %collective-permute-start.1 = (bf16[1,1,2,384,128]{4,3,2,0,1:T(8,128)(2,1)}, bf16[1,1,2,384,128]{4,3,2,0,1:T(8,128)(2,1)}, u32[]{:S(2)}, u32[]{:S(2)}) collective-permute-start(bf16[1,1,2,384,128]{4,3,2,0,1:T(8,128)(2,1)} %get-tuple-element.40), channel_id=1, source_target_pairs={{0,8},{4,12},{8,16},{12,20},{16,24},{20,28},{24,0},{28,4},{1,9},{5... | collective-permute-start | bytes 589832 | tf_op jit(solution)/shard_map/ppermute | solution.py:28
  30.0 20.2 %collective-permute-start.2 = (bf16[1,1,2,384,128]{4,3,2,0,1:T(8,128)(2,1)}, bf16[1,1,2,384,128]{4,3,2,0,1:T(8,128)(2,1)}, u32[]{:S(2)}, u32[]{:S(2)}) collective-permute-start(bf16[1,1,2,384,128]{4,3,2,0,1:T(8,128)(2,1)} %get-tuple-element.39), channel_id=1, source_target_pairs={{0,12},{4,16},{8,20},{12,24},{16,28},{20,0},{24,4},{28,8},{1,13},{... | collective-permute-start | bytes 589832 | tf_op jit(solution)/shard_map/ppermute | solution.py:28
  32.7 20.5 %collective-permute-start.3 = (bf16[1,1,2,384,128]{4,3,2,0,1:T(8,128)(2,1)}, bf16[1,1,2,384,128]{4,3,2,0,1:T(8,128)(2,1)S(1)}, u32[]{:S(2)}, u32[]{:S(2)}) collective-permute-start(bf16[1,1,2,384,128]{4,3,2,0,1:T(8,128)(2,1)} %get-tuple-element.38), channel_id=1, source_target_pairs={{0,16},{4,20},{8,24},{12,28},{16,0},{20,4},{24,8},{28,12},{1,17},{... | collective-permute-start | bytes 589832 | tf_op jit(solution)/shard_map/ppermute | solution.py:28
  34.3 19.0 %collective-permute-start.4 = (bf16[1,1,2,384,128]{4,3,2,0,1:T(8,128)(2,1)}, bf16[1,1,2,384,128]{4,3,2,0,1:T(8,128)(2,1)S(1)}, u32[]{:S(2)}, u32[]{:S(2)}) collective-permute-start(bf16[1,1,2,384,128]{4,3,2,0,1:T(8,128)(2,1)} %get-tuple-element.37), channel_id=1, source_target_pairs={{0,20},{4,24},{8,28},{12,0},{16,4},{20,8},{24,12},{28,16},{1,21},{... | collective-permute-start | bytes 589832 | tf_op jit(solution)/shard_map/ppermute | solution.py:28
  36.6 16.7 %collective-permute-start.5 = (bf16[1,1,2,384,128]{4,3,2,0,1:T(8,128)(2,1)}, bf16[1,1,2,384,128]{4,3,2,0,1:T(8,128)(2,1)S(1)}, u32[]{:S(2)}, u32[]{:S(2)}) collective-permute-start(bf16[1,1,2,384,128]{4,3,2,0,1:T(8,128)(2,1)} %get-tuple-element.36), channel_id=1, source_target_pairs={{0,24},{4,28},{8,0},{12,4},{16,8},{20,12},{24,16},{28,20},{1,25},{... | collective-permute-start | bytes 589832 | tf_op jit(solution)/shard_map/ppermute | solution.py:28
  38.3 16.4 %collective-permute-start.6 = (bf16[1,1,2,384,128]{4,3,2,0,1:T(8,128)(2,1)}, bf16[1,1,2,384,128]{4,3,2,0,1:T(8,128)(2,1)S(1)}, u32[]{:S(2)}, u32[]{:S(2)}) collective-permute-start(bf16[1,1,2,384,128]{4,3,2,0,1:T(8,128)(2,1)} %get-tuple-element.35), channel_id=1, source_target_pairs={{0,28},{4,0},{8,4},{12,8},{16,12},{20,16},{24,20},{28,24},{1,29},{... | collective-permute-start | bytes 589832 | tf_op jit(solution)/shard_map/ppermute | solution.py:28
  172.5 1.0 copy-start.3
  271.6 40.2 %copy-start.2 = (f32[512,512]{1,0:T(8,128)}, f32[512,512]{1,0:T(8,128)S(1)}, u32[]{:S(2)}) copy-start(f32[512,512]{1,0:T(8,128)S(1)} %get-tuple-element.105) | copy-start | bytes 3145732
  311.8 2.1 copy-start.4
  314.3 3.9 %copy-start.5 = (f32[4,128,128]{1,2,0:T(8,128)S(1)}, f32[4,128,128]{1,2,0:T(8,128)}, u32[]{:S(2)}) copy-start(f32[4,128,128]{1,2,0:T(8,128)} %copy-done.4) | copy-start | bytes 786436
Sparse Core Ops, SparseCore 0:
  71.8 95.7 all-reduce.2
